TPU v7x, 16 devices: a whole 2x2x2 slice. The times are simulated.
16 devices in a mesh: dp: 1, ep: 16 (over x, y, z, core).
Axes of the slice: x: 2, y: 2, z: 2, core: 2. Of those that a mesh axis runs over, the one named last changes fastest.
Arguments:
- x: bfloat16 [1, 16, 256, 3584], P('dp', 'ep')
- expert: int32 [1, 16, 256, 8], P('dp', 'ep')
- slot: int32 [1, 16, 256, 8], P('dp', 'ep')
- gate: float32 [1, 16, 256, 8], P('dp', 'ep')
- w_gate: bfloat16 [32, 3584, 2560], P('ep')
- w_up: bfloat16 [32, 3584, 2560], P('ep')
- w_down: bfloat16 [32, 2560, 3584], P('ep')
- s_gate: bfloat16 [3584, 20480], replicated
- s_up: bfloat16 [3584, 20480], replicated
- s_down: bfloat16 [20480, 3584], replicated
Outputs:
- y: bfloat16 [1, 16, 256, 3584], P('dp', 'ep')
All inputs are finite; a program needn't handle non-finite values.
Results may differ from a plain program's by a relative error of at most 0.009.
Values are sent between devices in bfloat16 or wider.
A program may use at most 2 GiB of HBM per device.

v0:
```python
import jax
import jax.numpy as jnp
from jax import lax
from jax.sharding import NamedSharding, PartitionSpec as P


def einsum(form, a, b):
    return jnp.einsum(form, a.astype(jnp.float32), b.astype(jnp.float32))


def for_all(x, s_gate, s_up, s_down):
    h = jax.nn.silu(einsum("...d,df->...f", x, s_gate)) * einsum("...d,df->...f", x, s_up)
    return einsum("...f,fd->...d", h.astype(jnp.bfloat16), s_down)


def solution(mesh):
    def placed(v, *spec):
        return lax.with_sharding_constraint(v, NamedSharding(mesh, P(*spec)))

    def step(x, expert, slot, gate, w_gate, w_up, w_down, s_gate, s_up, s_down):
        experts, (tokens, top) = w_gate.shape[0], expert.shape[2:]
        slots = 5 * tokens * top // (4 * experts)
        to_expert = jax.nn.one_hot(expert, experts, dtype=jnp.bfloat16)
        to_slot = jax.nn.one_hot(slot, slots, dtype=jnp.bfloat16)
        weighted = to_expert * gate[..., None].astype(jnp.bfloat16)
        dispatch = einsum("abtke,abtkc->abtec", to_expert, to_slot).astype(jnp.bfloat16)
        combine = einsum("abtke,abtkc->abtec", weighted, to_slot).astype(jnp.bfloat16)
        z = einsum("abtec,abtd->aebcd", dispatch, x).astype(jnp.bfloat16)
        z = placed(z, "dp", None, "ep", None, None)
        z = placed(z, "dp", "ep", None, None, None)
        h = jax.nn.silu(einsum("aebcd,edf->aebcf", z, w_gate))
        h = (h * einsum("aebcd,edf->aebcf", z, w_up)).astype(jnp.bfloat16)
        out = einsum("aebcf,efd->aebcd", h, w_down).astype(jnp.bfloat16)
        out = placed(out, "dp", "ep", None, None, None)
        out = placed(out, "dp", None, "ep", None, None)
        y = einsum("abtec,aebcd->abtd", combine, out)
        return (y + for_all(x, s_gate, s_up, s_down)).astype(jnp.bfloat16)

    return step
```

profile of v0, /device:TPU:0, one launch (start us, length us, event | category | flops | bytes accessed | tf_op | source)
XLA Modules:
  0.0 785.0 jit_solution(9056133563951313477)
XLA Ops:
  0.0 0.0 copy-start
  0.0 1.0 copy.11
  1.0 0.8 copy.9
  1.8 3.5 convolution_convert_fusion.2
  5.3 0.0 copy-done
  5.3 12.5 %convolution_convert_fusion = bf16[32,80,3584]{2,1,0:T(8,128)(2,1)} fusion(bf16[256,32,80]{2,1,0:T(8,128)(2,1)} %convolution_convert_fusion.2, bf16[1,1,256,3584]{3,2,1,0:T(8,128)(2,1)S(1)} %copy-done), kind=kOutput, calls=%fused_computation.24 | convolution fusion | flops 4706795520 | bytes 21495808 | tf_op jit(solution)/abtec,abtd->aebcd/dot_general | solution.py:8
  17.7 0.0 copy-start.1
  17.7 5.3 all-to-all-start
  23.0 0.0 copy-done.1
  23.1 0.1 copy.10
  23.2 3.9 convolution_convert_fusion.1
  27.1 63.2 %convolution_bitcast_fusion.1 = f32[1,256,20480]{2,1,0:T(8,128)} fusion(bf16[3584,20480]{1,0:T(8,128)(2,1)} %param.7, bf16[1,1,256,3584]{3,2,1,0:T(8,128)(2,1)S(1)} %copy-done), kind=kOutput, calls=%fused_computation.7 | convolution fusion | flops 37580963840 | bytes 169607168 | tf_op jit(solution)/...d,df->...f/dot_general | solution.py:8
  90.4 208.6 %all-to-all-done = bf16[1,16,2,1,80,3584]{5,4,2,3,0,1:T(8,128)(2,1)} async-done(((bf16[1,16,2,1,80,3584]{5,4,2,3,0,1:T(8,128)(2,1)}), bf16[1,16,2,1,80,3584]{5,4,2,3,0,1:T(8,128)(2,1)}, u32[]{:S(2)}, u32[]{:S(2)}) %all-to-all-start) | async-done | bytes 18350112 | tf_op jit(solution)/sharding_constraint;jit(solution)/sharding_constraint | solution.py:18
  299.0 57.4 %fusion.2 = f32[2,16,80,2560]{3,2,1,0:T(8,128)} fusion(bf16[2,3584,2560]{2,1,0:T(8,128)(2,1)} %param.5, bf16[1,16,2,1,80,3584]{5,4,2,3,0,1:T(8,128)(2,1)} %all-to-all-done), kind=kOutput, calls=%fused_computation.2 | convolution fusion | flops 46976204800 | bytes 81264640 | tf_op jit(solution)/aebcd,edf->aebcf/dot_general | solution.py:8
  356.4 60.7 %fusion.7 = bf16[1,2,16,80,2560]{4,3,2,1,0:T(8,128)(2,1)} fusion(f32[2,16,80,2560]{3,2,1,0:T(8,128)} %fusion.2, bf16[2,3584,2560]{2,1,0:T(8,128)(2,1)} %param.4, bf16[1,16,2,1,80,3584]{5,4,2,3,0,1:T(8,128)(2,1)} %all-to-all-done), kind=kOutput, calls=%fused_computation.10 | convolution fusion | flops 47015526400 | bytes 94371840 | tf_op jit(solution)/aebcd,edf->aebcf/dot_general | solution.py:8
  417.1 56.1 %convert_bitcast_fusion = bf16[1,2,16,1,80,3584]{5,4,2,1,3,0:T(8,128)(2,1)} fusion(bf16[2,2560,3584]{2,1,0:T(8,128)(2,1)} %param.6, bf16[1,2,16,80,2560]{4,3,2,1,0:T(8,128)(2,1)} %fusion.7), kind=kOutput, calls=%fused_computation.20 | convolution fusion | flops 46985379840 | bytes 68157440 | tf_op jit(solution)/aebcf,efd->aebcd/dot_general | solution.py:8
  473.2 15.7 %copy.15 = bf16[1,2,16,1,80,3584]{5,4,1,3,0,2:T(8,128)(2,1)} copy(bf16[1,2,16,1,80,3584]{5,4,2,1,3,0:T(8,128)(2,1)} %convert_bitcast_fusion) | data formatting | bytes 36700160 | tf_op jit(solution)/sharding_constraint;jit(solution)/sharding_constraint | solution.py:18
  488.9 4.6 all-to-all-start.1
  493.5 63.2 %fusion.72 = bf16[256,20480]{1,0:T(8,128)(2,1)} fusion(bf16[3584,20480]{1,0:T(8,128)(2,1)} %param.8, bf16[1,1,256,3584]{3,2,1,0:T(8,128)(2,1)S(1)} %copy-done, f32[1,256,20480]{2,1,0:T(8,128)} %convolution_bitcast_fusion.1), kind=kOutput, calls=%bitcast_fusion.clone.1 | convolution fusion | flops 37612421120 | bytes 180092928 | tf_op jit(solution)/...d,df->...f/dot_general | solution.py:8
  556.7 55.7 %fusion.49 = f32[256,3584]{1,0:T(8,128)} fusion(bf16[20480,3584]{1,0:T(8,128)(2,1)} %param.9, bf16[256,20480]{1,0:T(8,128)(2,1)} %fusion.72), kind=kOutput, calls=%fused_computation.50 | convolution fusion | flops 37580963840 | bytes 160956416 | tf_op jit(solution)/...f,fd->...d/dot_general | solution.py:8
  612.4 156.8 %all-to-all-done.1 = bf16[1,2,16,1,80,3584]{5,4,1,3,0,2:T(8,128)(2,1)} async-done(((bf16[1,2,16,1,80,3584]{5,4,1,3,0,2:T(8,128)(2,1)}), bf16[1,2,16,1,80,3584]{5,4,1,3,0,2:T(8,128)(2,1)}, u32[]{:S(2)}, u32[]{:S(2)}) %all-to-all-start.1) | async-done | bytes 18350112 | tf_op jit(solution)/sharding_constraint;jit(solution)/sharding_constraint | solution.py:18
  769.3 15.3 %fusion.28 = bf16[1,1,256,3584]{3,2,1,0:T(8,128)(2,1)} fusion(f32[256,3584]{1,0:T(8,128)} %fusion.49, bf16[32,80,3584]{2,1,0:T(8,128)(2,1)} %bitcast.38, bf16[256,32,80]{2,1,0:T(8,128)(2,1)} %convolution_convert_fusion.1), kind=kOutput, calls=%fused_computation.28 | convolution fusion | flops 4699455488 | bytes 25165824 | tf_op jit(solution)/abtec,aebcd->abtd/dot_general | solution.py:8
  (1 shorter events, 0.0 us)
Async XLA Ops:
  0.0 5.3 copy-start
  17.7 5.3 copy-start.1
  17.7 281.2 %all-to-all-start = ((bf16[1,16,2,1,80,3584]{5,4,2,3,0,1:T(8,128)(2,1)}), bf16[1,16,2,1,80,3584]{5,4,2,3,0,1:T(8,128)(2,1)}, u32[]{:S(2)}, u32[]{:S(2)}) async-start(bf16[1,16,2,1,80,3584]{5,4,2,3,0,1:T(8,128)(2,1)} %bitcast.165), calls=%async_computation | async-start | bytes 36700160 | tf_op jit(solution)/sharding_constraint;jit(solution)/sharding_constraint | solution.py:18
  488.9 280.4 %all-to-all-start.1 = ((bf16[1,2,16,1,80,3584]{5,4,1,3,0,2:T(8,128)(2,1)}), bf16[1,2,16,1,80,3584]{5,4,1,3,0,2:T(8,128)(2,1)}, u32[]{:S(2)}, u32[]{:S(2)}) async-start(bf16[1,2,16,1,80,3584]{5,4,1,3,0,2:T(8,128)(2,1)} %copy.15), calls=%async_computation.1 | async-start | bytes 36700160 | tf_op jit(solution)/sharding_constraint;jit(solution)/sharding_constraint | solution.py:18
where the time goes:
time: 793 us; the launch traced here: 785 us
  matrix products  392 us (49%)
  waiting for transfers between devices  365 us (46%)
  local copies, waits for them, and re-layouts  17.6 us (2%)
  starting transfers between devices  9.92 us (1%)
    dot_general x10, matrix products, einsum(): return jnp.einsum(form, a.astype(jnp.float32), b.astype(jnp.float32))  392 us
    another operation x2, waiting for transfers between devices, placed(): return lax.with_sharding_constraint(v, NamedSharding(mesh, P(*spec)))  365 us
  transfers between devices with their start and end apart: 2, of which 2 were waited for; matrix products, arithmetic and copies ran while one was open for 24% of the time, Pallas kernels for 0%

commit v1 on v0

v1 whole, which is shorter than its diff:
```python
import functools

import jax
import jax.numpy as jnp
from jax import lax
from jax.experimental import pallas as pl
from jax.experimental.pallas import tpu as pltpu
from jax.sharding import PartitionSpec as P


D = 3584
FF = 2560
SFF = 20480
TOP = 8
SLOTS = 80
NDEV = 16
CHIPS = 8
TOK = 256
CHUNKS = 2
CT = TOK // CHUNKS
GROUP = 8
WIN = SLOTS + 16
CAP = NDEV * SLOTS
ZROWS = CAP + 96
PASS = 6
FB = 512
NB = FF // FB
SB = 512
SA_BLOCKS = 19
VMEM = 64 * 1024 * 1024 - 65536


def shared_kernel(x_ref, wg_ref, wu_ref, wd_ref, acc_in, acc_ref, *, first):
    j = pl.program_id(0)

    @pl.when(j == 0)
    def _():
        if first:
            acc_ref[...] = jnp.zeros_like(acc_ref)
        else:
            acc_ref[...] = acc_in[...]

    x = x_ref[...]
    g = jnp.dot(x, wg_ref[...], preferred_element_type=jnp.float32)
    u = jnp.dot(x, wu_ref[...], preferred_element_type=jnp.float32)
    h = (jax.nn.silu(g) * u).astype(jnp.bfloat16)
    acc_ref[...] += jnp.dot(h, wd_ref[...], preferred_element_type=jnp.float32)


def shared(x, wg, wu, wd, start, count, acc=None):
    first = acc is None
    rows = x.shape[0]
    if first:
        acc = jnp.zeros((8, 128), jnp.float32)
        acc_spec = pl.BlockSpec((8, 128), lambda j: (0, 0))
    else:
        acc_spec = pl.BlockSpec((rows, D), lambda j: (0, 0))
    return pl.pallas_call(
        functools.partial(shared_kernel, first=first),
        grid=(count,),
        in_specs=[
            pl.BlockSpec((rows, D), lambda j: (0, 0)),
            pl.BlockSpec((D, SB), lambda j: (0, start + j)),
            pl.BlockSpec((D, SB), lambda j: (0, start + j)),
            pl.BlockSpec((SB, D), lambda j: (start + j, 0)),
            acc_spec,
        ],
        out_specs=pl.BlockSpec((rows, D), lambda j: (0, 0)),
        out_shape=jax.ShapeDtypeStruct((rows, D), jnp.float32),
        compiler_params=pltpu.CompilerParams(vmem_limit_bytes=VMEM),
        cost_estimate=pl.CostEstimate(
            flops=6 * rows * D * SB * count, bytes_accessed=6 * D * SB * count, transcendentals=rows * SB * count
        ),
        name="shared",
    )(x, wg, wu, wd, acc)


def routed_kernel(
    base_ref, off_ref, tiles_ref, core_ref, x_hbm, meta_ref, wg_ref, wu_ref, wd_ref, keep_hbm, away_hbm,
    zbuf, acc, xbuf, abuf, xsem, ksem, asem
):
    e, p, j = pl.program_id(0), pl.program_id(1), pl.program_id(2)
    mc = core_ref[0]

    def source(k, away):
        return 2 * k + (1 - mc if away else mc)

    def fetch(a, slot):
        return pltpu.make_async_copy(x_hbm.at[a], xbuf.at[slot], xsem.at[slot])

    @pl.when((e == 0) & (p == 0) & (j == 0))
    def _():
        fetch(0, 0).start()
        zbuf[...] = jnp.zeros_like(zbuf)

        def step(a, c):
            slot = lax.rem(a, 2)

            @pl.when(a < NDEV - 1)
            def _():
                fetch(a + 1, 1 - slot).start()

            fetch(a, slot).wait()
            m = meta_ref[a]
            rows = lax.broadcasted_iota(jnp.int32, (WIN, CT), 0).astype(jnp.float32)
            for q in range(2):
                pick = jnp.where(m[q : q + 1, :] == rows, 1.0, 0.0).astype(jnp.bfloat16)
                new = jnp.dot(pick, xbuf[slot], preferred_element_type=jnp.float32)
                base = pl.multiple_of(base_ref[q, a], 16)
                row = lax.broadcasted_iota(jnp.int32, (16, 1), 0)
                old = zbuf[q, pl.ds(base, 16), :].astype(jnp.float32)
                zbuf[q, pl.ds(base, 16), :] = jnp.where(row < off_ref[q, a], old, new[:16]).astype(jnp.bfloat16)
                zbuf[q, pl.ds(base + 16, WIN - 16), :] = new[16:].astype(jnp.bfloat16)
            return c

        lax.fori_loop(0, NDEV, step, 0)

    first = p * PASS * 128

    def ffn(start, size):
        z = zbuf[e, pl.ds(pl.multiple_of(first + start, 128), size), :]
        g = jnp.dot(z, wg_ref[0], preferred_element_type=jnp.float32)
        u = jnp.dot(z, wu_ref[0], preferred_element_type=jnp.float32)
        h = (jax.nn.silu(g) * u).astype(jnp.bfloat16)
        acc[pl.ds(start, size), :] += jnp.dot(h, wd_ref[0], preferred_element_type=jnp.float32)

    n = jnp.clip(tiles_ref[e] - p * PASS, 0, PASS)

    @pl.when(j == 0)
    def _():
        def clear(r, c):
            acc[pl.ds(pl.multiple_of(r * 128, 128), 128), :] = jnp.zeros((128, D), jnp.float32)
            return c

        lax.fori_loop(0, n, clear, 0)

    def big(r, c):
        ffn(pl.multiple_of(r * 512, 512), 512)
        return c

    lax.fori_loop(0, n // 4, big, 0)

    @pl.when(lax.rem(n // 2, 2) == 1)
    def _():
        ffn(pl.multiple_of(n // 4 * 512, 128), 256)

    @pl.when(lax.rem(n, 2) == 1)
    def _():
        ffn(pl.multiple_of((n - 1) * 128, 128), 128)

    @pl.when(j == NB - 1)
    def _():
        def keep(r, c):
            rows = acc[pl.ds(pl.multiple_of(r * 128, 128), 128), :]
            zbuf[e, pl.ds(pl.multiple_of(first + r * 128, 128), 128), :] = rows.astype(jnp.bfloat16)
            return c

        lax.fori_loop(0, n, keep, 0)

    @pl.when((e == 1) & (p == 1) & (j == NB - 1))
    def _():
        rows = lax.broadcasted_iota(jnp.int32, (WIN, CT), 0).astype(jnp.float32)

        def put_keep(k, slot):
            return pltpu.make_async_copy(acc.at[pl.ds(slot * CT, CT)], keep_hbm.at[k], ksem.at[slot])

        def put_away(k, slot):
            return pltpu.make_async_copy(abuf.at[slot], away_hbm.at[k], asem.at[slot])

        def result(a):
            m = meta_ref[a]
            total = None
            for q in range(2):
                w = jnp.where(m[q : q + 1, :] == rows, m[2 + q : 3 + q, :], 0.0).astype(jnp.bfloat16)
                base = pl.multiple_of(base_ref[q, a], 16)
                t = lax.dot_general(
                    w, zbuf[q, pl.ds(base, WIN), :], (((0,), (0,)), ((), ())), preferred_element_type=jnp.float32
                )
                total = t if total is None else total + t
            return total

        def step(k, c):
            slot = lax.rem(k, 2)

            @pl.when(k >= 2)
            def _():
                put_away(k - 2, slot).wait()
                put_keep(k - 2, slot).wait()

            abuf[slot] = result(source(k, True)).astype(jnp.bfloat16)
            put_away(k, slot).start()
            acc[pl.ds(pl.multiple_of(slot * CT, CT), CT), :] = result(source(k, False))
            put_keep(k, slot).start()
            return c

        lax.fori_loop(0, CHIPS, step, 0)
        for k in (CHIPS - 2, CHIPS - 1):
            put_away(k, k % 2).wait()
            put_keep(k, k % 2).wait()


def block(e, p, j, tiles):
    return jnp.where(tiles[e] > p * PASS, j, NB - 1)


def routed(base, off, tiles, core, x_all, meta, wg, wu, wd):
    grid_spec = pltpu.PrefetchScalarGridSpec(
        num_scalar_prefetch=4,
        grid=(2, 2, NB),
        in_specs=[
            pl.BlockSpec(memory_space=pl.ANY),
            pl.BlockSpec((NDEV, 8, CT), lambda e, p, j, *_: (0, 0, 0)),
            pl.BlockSpec((1, D, FB), lambda e, p, j, b, o, t, c: (e, 0, block(e, p, j, t))),
            pl.BlockSpec((1, D, FB), lambda e, p, j, b, o, t, c: (e, 0, block(e, p, j, t))),
            pl.BlockSpec((1, FB, D), lambda e, p, j, b, o, t, c: (e, block(e, p, j, t), 0)),
        ],
        out_specs=[pl.BlockSpec(memory_space=pl.ANY), pl.BlockSpec(memory_space=pl.ANY)],
        scratch_shapes=[
            pltpu.VMEM((2, ZROWS, D), jnp.bfloat16),
            pltpu.VMEM((PASS * 128, D), jnp.float32),
            pltpu.VMEM((2, CT, D), jnp.bfloat16),
            pltpu.VMEM((2, CT, D), jnp.bfloat16),
            pltpu.SemaphoreType.DMA((2,)),
            pltpu.SemaphoreType.DMA((2,)),
            pltpu.SemaphoreType.DMA((2,)),
        ],
    )
    return pl.pallas_call(
        routed_kernel,
        grid_spec=grid_spec,
        out_shape=[
            jax.ShapeDtypeStruct((CHIPS, CT, D), jnp.float32),
            jax.ShapeDtypeStruct((CHIPS, CT, D), jnp.bfloat16),
        ],
        compiler_params=pltpu.CompilerParams(vmem_limit_bytes=VMEM),
        cost_estimate=pl.CostEstimate(
            flops=6 * 1280 * D * FF, bytes_accessed=12 * D * FF, transcendentals=1280 * FF
        ),
        name="routed",
    )(base, off, tiles, core, x_all, meta, wg, wu, wd)


def positions(codes, gates, me):
    out = []
    mine = (2 * me + jnp.arange(2)).astype(jnp.float32)
    hit = codes[:, None].astype(jnp.float32) == mine[None, :, None, None, None]
    chosen = jnp.sum(hit.astype(jnp.float32), axis=2)
    weight = jnp.sum(jnp.where(hit, gates[:, None].astype(jnp.float32), 0.0), axis=2)
    before = jnp.triu(jnp.ones((CT, CT), jnp.bfloat16), 1)
    rank = jnp.einsum(
        "aect,tu->aecu", chosen.astype(jnp.bfloat16), before, preferred_element_type=jnp.float32
    )
    count = jnp.sum(chosen, axis=3).astype(jnp.int32)
    end = jnp.cumsum(count, axis=0)
    begin = end - count
    off = lax.rem(begin, 16)
    base = begin - off
    pos = jnp.where(chosen > 0, rank + off[..., None].astype(jnp.float32), -1.0)
    tiles = (end[-1] + 127) // 128
    for c in range(CHUNKS):
        meta = jnp.concatenate(
            [pos[:, :, c], weight[:, :, c], jnp.zeros((NDEV, 4, CT), jnp.float32)], axis=1
        )
        out.append((base[:, :, c].T, off[:, :, c].T, tiles[:, c], meta))
    return out


def solution(mesh):
    def layer(x, expert, slot, gate, w_gate, w_up, w_down, s_gate, s_up, s_down):
        x, expert, slot, gate = x[0, 0], expert[0, 0], slot[0, 0], gate[0, 0]
        me = lax.axis_index("ep")
        core = lax.rem(me, 2)
        chip = me // 2

        code = jnp.where(slot < SLOTS, expert, 32).astype(jnp.bfloat16)
        packed = jnp.concatenate([code, gate.astype(jnp.bfloat16)], axis=1)
        packed = packed.reshape(TOK // (GROUP * CHUNKS), CHUNKS, GROUP, 2 * TOP)
        packed = packed.transpose(3, 1, 0, 2).reshape(2 * TOP, TOK)
        allm = lax.all_gather(packed, "ep", axis=0).reshape(NDEV, 2 * TOP, CHUNKS, CT)
        plan = positions(allm[:, :TOP], allm[:, TOP:], me)

        xs = x.reshape(TOK // (GROUP * CHUNKS), CHUNKS, GROUP, D)
        gathered = [
            lax.all_gather(xs[:, c].reshape(CT, D), "ep", axis=0) for c in range(CHUNKS)
        ]
        acc = shared(x, s_gate, s_up, s_down, 0, SA_BLOCKS)
        parts = []
        pair = [(i, i ^ 1) for i in range(NDEV)]
        groups = [[2 * k + c for k in range(CHIPS)] for c in range(2)]
        after = acc
        for c in range(CHUNKS):
            base, off, tiles, meta = plan[c]
            tokens, after = lax.optimization_barrier((gathered[c], after))
            if c == 0:
                acc = after
            else:
                parts[-1] = (parts[-1][0], after)
            keep, away = routed(base, off, tiles, core[None], tokens, meta, w_gate, w_up, w_down)
            got = lax.ppermute(away, "ep", pair)
            total = (keep + got.astype(jnp.float32)).astype(jnp.bfloat16)
            own = lax.dynamic_index_in_dim(keep, chip, 0, keepdims=False)
            own = own + lax.dynamic_index_in_dim(got, chip, 0, keepdims=False).astype(jnp.float32)
            parts.append((own, total))
            after = total
        x, acc, last = lax.optimization_barrier((x, acc, after))
        parts[-1] = (parts[-1][0], last)
        for c in range(CHUNKS):
            back = lax.all_to_all(parts[c][1], "ep", 0, 0, axis_index_groups=groups, tiled=True)
            parts[c] = (parts[c][0], back)
        rest = shared(x, s_gate, s_up, s_down, SA_BLOCKS, SFF // SB - SA_BLOCKS, acc)
        rest = rest.reshape(TOK // (GROUP * CHUNKS), CHUNKS, GROUP, D)
        outs = []
        others = (jnp.arange(CHIPS) != chip)[:, None, None]
        for c in range(CHUNKS):
            own, back = parts[c]
            t = own + jnp.sum(jnp.where(others, back.astype(jnp.float32), 0.0), axis=0)
            outs.append(t.reshape(TOK // (GROUP * CHUNKS), GROUP, D) + rest[:, c])
        y = jnp.stack(outs, axis=1).reshape(TOK, D).astype(jnp.bfloat16)
        return y[None, None]

    row = P("dp", "ep", None, None)
    return jax.shard_map(
        layer,
        mesh=mesh,
        in_specs=(row, row, row, row) + (P("ep", None, None),) * 3 + (P(None, None),) * 3,
        out_specs=row,
        check_vma=False,
    )
```

time: 793 us -> 619 us (0.78)
  Pallas kernels: 0 us -> 411 us
  matrix products: 392 us -> 0.13 us
  waiting for transfers between devices: 365 us -> 113 us
  other arithmetic: 0.01 us -> 39.4 us
  blocking collectives: 0 us -> 15.5 us
  between operations: 0.56 us -> 13.6 us
  local copies, waits for them, and re-layouts: 17.6 us -> 9.46 us
    pallas_call x0 -> x4, Pallas kernels: none -> 411 us  [the longest x2 244 us: routed(): pl.pallas_call(routed_kernel, grid_spec=grid_spec, out_shape=[jax.ShapeDt...]
    dot_general x10 -> x1, matrix products: 392 us -> 0.13 us  [positions(): jnp.einsum('aect,tu->aecu', chosen.astype(jnp.bfloat16), before, preferre...]
    another operation x2 -> x0, waiting for transfers between devices: 365 us -> none  [placed(): return lax.with_sharding_constraint(v, NamedSharding(mesh, P(*spec)))]
    all_to_all x0 -> x2, waiting for transfers between devices: none -> 99 us  [layer(): lax.all_to_all(parts[c][1], 'ep', 0, 0, axis_index_groups=groups, tiled=T...]
    convert_element_type x1 -> x9, other arithmetic: 0.01 us -> 20.5 us  [the longest x2 19 us: layer(): total = (keep + got.astype(jnp.float32)).astype(jnp.bfloat16)]
    all_gather x0 -> x1, blocking collectives: none -> 15.5 us  [layer(): lax.all_gather(packed, 'ep', axis=0).reshape(NDEV, 2 * TOP, CHUNKS, CT)]
    all_to_all x0 -> x2, starting transfers between devices: none -> 15.5 us  [layer(): lax.all_to_all(parts[c][1], 'ep', 0, 0, axis_index_groups=groups, tiled=T...]
    ppermute x0 -> x2, waiting for transfers between devices: none -> 13.5 us  [layer(): got = lax.ppermute(away, 'ep', pair)]
  transfers between devices with their start and end apart: 2 -> 6, of which waited for: 2 -> 4; matrix products, arithmetic and copies ran while one was open for 24% -> 4% of each run, Pallas kernels for 0% -> 46%
where the time goes in v1:
time: 619 us; the launch traced here: 618 us
  Pallas kernels  411 us (66%)
  waiting for transfers between devices  113 us (18%)
  other arithmetic  39.4 us (6%)
  starting transfers between devices  15.6 us (3%)
  blocking collectives  15.5 us (3%)
  between operations  13.6 us (2%)
  local copies, waits for them, and re-layouts  9.46 us (2%)
    pallas_call x2, Pallas kernels, routed(): pl.pallas_call(routed_kernel, grid_spec=grid_spec, out_shape=[jax.ShapeDt...  244 us
    pallas_call x2, Pallas kernels, shared(): pl.pallas_call(functools.partial(shared_kernel, first=first), grid=(count...  167 us
    all_to_all x2, waiting for transfers between devices, layer(): lax.all_to_all(parts[c][1], 'ep', 0, 0, axis_index_groups=groups, tiled=T...  99 us
    convert_element_type x2, other arithmetic, layer(): total = (keep + got.astype(jnp.float32)).astype(jnp.bfloat16)  19 us
    all_gather x1, blocking collectives, layer(): lax.all_gather(packed, 'ep', axis=0).reshape(NDEV, 2 * TOP, CHUNKS, CT)  15.5 us
    all_to_all x2, starting transfers between devices, layer(): lax.all_to_all(parts[c][1], 'ep', 0, 0, axis_index_groups=groups, tiled=T...  15.5 us
    ppermute x2, waiting for transfers between devices, layer(): got = lax.ppermute(away, 'ep', pair)  13.5 us
  transfers between devices with their start and end apart: 6, of which 4 were waited for; matrix products, arithmetic and copies ran while one was open for 4% of the time, Pallas kernels for 46%

profile of v1, /device:TPU:0, one launch (start us, length us, event | category | flops | bytes accessed | tf_op | source)
XLA Modules:
  0.0 617.9 jit_solution(8233524446404555816)
XLA Ops:
  6.5 2.8 slice_bitcast_fusion
  9.4 0.7 all-gather.5.cloned.1.call-update
  10.1 0.7 convert_element_type.105
  10.8 0.1 convert_element_type.106
  11.0 0.7 select_convert_fusion
  11.8 0.2 maximum_bitcast_fusion
  12.0 0.2 copy.82
  12.3 15.5 %all_gather.9 = bf16[16,16,256]{2,1,0:T(8,128)(2,1)S(1)} all-gather(bf16[1,16,256]{2,1,0:T(8,128)(2,1)S(1)} %copy.83), channel_id=1, replica_groups=mesh['dp'=1,'ep'=16] {'ep'}, dimensions={0}, use_global_device_ids=true | all-gather | bytes 139264 | tf_op jit(solution)/shard_map/all_gather | solution.py:279
  28.0 0.4 convert_reduce_fusion
  28.9 0.8 slice_reduce_fusion.1
  29.6 0.6 fusion.18
  30.2 0.6 fusion.19
  30.8 0.1 fusion.5
  31.1 0.7 maximum_maximum_fusion.1
  31.9 0.6 broadcast_in_dim.58.acc_in
  32.4 81.2 %shared.2.acc_in = f32[256,3584]{1,0:T(8,128)} custom-call(bf16[256,3584]{1,0:T(8,128)(2,1)} %bitcast.73, bf16[3584,20480]{1,0:T(8,128)(2,1)} %wg_ref.7, bf16[3584,20480]{1,0:T(8,128)(2,1)} %wu_ref.7, bf16[20480,3584]{1,0:T(8,128)(2,1)} %wd_ref.7, f32[8,128]{1,0:T(8,128)} %broadcast_in_dim.58.acc_in), custom_call_target="tpu_custom_call" | custom-call | flops 53552873472 | bytes 209190912 | tf_op jit(solution)/shard_map/shared/pallas_call | solution.py:58
  113.6 118.6 %routed.2 = (f32[8,128,3584]{2,1,0:T(8,128)}, bf16[8,128,3584]{2,1,0:T(8,128)(2,1)}) custom-call(s32[2,16]{1,0:T(2,128)} %bitcast.82, s32[2,16]{1,0:T(2,128)} %bitcast.81, s32[2]{0:T(128)} %get-tuple-element.30.tiles_ref, s32[1]{0:T(128)} %bitcast.7.core_ref, bf16[16,128,3584]{2,1,0:T(8,128)(2,1)} %all-gather.3.cloned.1.call-done.x_hbm, ...), custom_call_target="tpu_custom_call" | custom-call | flops 70464307200 | bytes 110100480 | tf_op jit(solution)/shard_map/routed/pallas_call | solution.py:228
  232.3 11.9 %collective-permute-done = bf16[8,128,3584]{2,1,0:T(8,128)(2,1)S(1)} collective-permute-done((bf16[8,128,3584]{2,1,0:T(8,128)(2,1)}, bf16[8,128,3584]{2,1,0:T(8,128)(2,1)S(1)}, u32[]{:S(2)}, u32[]{:S(2)}) %collective-permute-start) | collective-permute-done | bytes 7340064 | tf_op jit(solution)/shard_map/ppermute | solution.py:299
  244.2 3.0 copy-done.1
  247.1 8.5 %add_convert_fusion.1 = bf16[8,128,3584]{2,1,0:T(8,128)(2,1)} fusion(f32[8,128,3584]{2,1,0:T(8,128)} %get-tuple-element.17, bf16[8,128,3584]{2,1,0:T(8,128)(2,1)S(1)} %collective-permute-done), kind=kLoop, calls=%fused_computation.3 | loop fusion | flops 11010048 | bytes 29360128 | tf_op jit(solution)/shard_map/convert_element_type | solution.py:300
  255.6 125.0 %routed.3 = (f32[8,128,3584]{2,1,0:T(8,128)}, bf16[8,128,3584]{2,1,0:T(8,128)(2,1)}) custom-call(s32[2,16]{1,0:T(2,128)} %bitcast.80, s32[2,16]{1,0:T(2,128)} %bitcast.79, s32[2]{0:T(128)} %get-tuple-element.31.tiles_ref, s32[1]{0:T(128)} %bitcast.7.core_ref, bf16[16,128,3584]{2,1,0:T(8,128)(2,1)} %all-gather.5.cloned.1.call-done.x_hbm, ...), custom_call_target="tpu_custom_call" | custom-call | flops 70464307200 | bytes 110100480 | tf_op jit(solution)/shard_map/routed/pallas_call | solution.py:228
  380.7 10.3 %all-to-all-start = ((bf16[8,128,3584]{2,1,0:T(8,128)(2,1)}), bf16[8,128,3584]{2,1,0:T(8,128)(2,1)}, u32[]{:S(2)}, u32[]{:S(2)}) async-start(bf16[8,128,3584]{2,1,0:T(8,128)(2,1)} %add_convert_fusion.1), calls=%async_computation | async-start | bytes 14680064 | tf_op jit(solution)/shard_map/all_to_all | solution.py:308
  391.0 1.6 collective-permute-done.1
  392.7 10.5 %add_convert_fusion = bf16[8,128,3584]{2,1,0:T(8,128)(2,1)} fusion(f32[8,128,3584]{2,1,0:T(8,128)} %get-tuple-element.22, bf16[8,128,3584]{2,1,0:T(8,128)(2,1)} %collective-permute-done.1), kind=kLoop, calls=%fused_computation.1 | loop fusion | flops 11010048 | bytes 29360128 | tf_op jit(solution)/shard_map/convert_element_type | solution.py:300
  403.2 87.7 %all-to-all-done = bf16[8,128,3584]{2,1,0:T(8,128)(2,1)} async-done(((bf16[8,128,3584]{2,1,0:T(8,128)(2,1)}), bf16[8,128,3584]{2,1,0:T(8,128)(2,1)}, u32[]{:S(2)}, u32[]{:S(2)}) %all-to-all-start) | async-done | bytes 7340064 | tf_op jit(solution)/shard_map/all_to_all | solution.py:308
  491.0 5.1 all-to-all-start.1
  496.1 0.5 iota_compare_fusion.1
  496.7 86.2 %shared.3 = f32[256,3584]{1,0:T(8,128)} custom-call(bf16[256,3584]{1,0:T(8,128)(2,1)} %bitcast.74, bf16[3584,20480]{1,0:T(8,128)(2,1)} %wg_ref.7, bf16[3584,20480]{1,0:T(8,128)(2,1)} %wu_ref.7, bf16[20480,3584]{1,0:T(8,128)(2,1)} %wd_ref.7, f32[256,3584]{1,0:T(8,128)} %shared.2.acc_in), custom_call_target="tpu_custom_call" | custom-call | flops 59190018048 | bytes 231211008 | tf_op jit(solution)/shard_map/shared/pallas_call | solution.py:58
  582.9 11.3 %all-to-all-done.1 = bf16[8,128,3584]{2,1,0:T(8,128)(2,1)} async-done(((bf16[8,128,3584]{2,1,0:T(8,128)(2,1)}), bf16[8,128,3584]{2,1,0:T(8,128)(2,1)}, u32[]{:S(2)}, u32[]{:S(2)}) %all-to-all-start.1) | async-done | bytes 7340064 | tf_op jit(solution)/shard_map/all_to_all | solution.py:308
  594.1 10.5 %select_reduce_fusion.1 = (f32[128,3584]{1,0:T(8,128)}, f32[128,3584]{1,0:T(8,128)}) fusion(bf16[8,128,3584]{2,1,0:T(8,128)(2,1)} %all-to-all-done, pred[8]{0:T(512)(128)(4,1)} %iota_compare_fusion.1, bf16[8,128,3584]{2,1,0:T(8,128)(2,1)} %all-to-all-done.1), kind=kLoop, calls=%fused_computation.2 | loop fusion | flops 21102592 | bytes 18350088 | tf_op jit(solution)/shard_map/reduce_sum | solution.py:316
  604.7 5.0 fusion.1
  609.7 1.4 pad_maximum_fusion
  (31 shorter events, 1.2 us)
Async XLA Ops:
  6.5 107.1 %all-gather.3.cloned.1.call-start = ((), (), s32[]{:S(2)}) async-start(), calls=%async_computation.2 | async-start | bytes 15597568 | tf_op jit(solution)/shard_map/all_gather | solution.py:284
  9.4 246.3 %all-gather.5.cloned.1.call-start = ((), (), s32[]{:S(2)}) async-start(), calls=%async_computation.3 | async-start | bytes 15597568 | tf_op jit(solution)/shard_map/all_gather | solution.py:284
  232.2 11.9 %collective-permute-start = (bf16[8,128,3584]{2,1,0:T(8,128)(2,1)}, bf16[8,128,3584]{2,1,0:T(8,128)(2,1)S(1)}, u32[]{:S(2)}, u32[]{:S(2)}) collective-permute-start(bf16[8,128,3584]{2,1,0:T(8,128)(2,1)} %get-tuple-element.18), channel_id=1, source_target_pairs={{0,1},{1,0},{2,3},{3,2},{4,5},{5,4},{6,7},{7,6},{8,9},{9,8},{10,11... | collective-permute-start | bytes 22020104 | tf_op jit(solution)/shard_map/ppermute | solution.py:299
  244.2 3.0 copy-start.1
  380.7 12.0 %collective-permute-start.1 = (bf16[8,128,3584]{2,1,0:T(8,128)(2,1)}, bf16[8,128,3584]{2,1,0:T(8,128)(2,1)}, u32[]{:S(2)}, u32[]{:S(2)}) collective-permute-start(bf16[8,128,3584]{2,1,0:T(8,128)(2,1)} %get-tuple-element.23), channel_id=1, source_target_pairs={{0,1},{1,0},{2,3},{3,2},{4,5},{5,4},{6,7},{7,6},{8,9},{9,8},{10,11... | collective-permute-start | bytes 22020104 | tf_op jit(solution)/shard_map/ppermute | solution.py:299
  380.7 110.3 %all-to-all-start = ((bf16[8,128,3584]{2,1,0:T(8,128)(2,1)}), bf16[8,128,3584]{2,1,0:T(8,128)(2,1)}, u32[]{:S(2)}, u32[]{:S(2)}) async-start(bf16[8,128,3584]{2,1,0:T(8,128)(2,1)} %add_convert_fusion.1), calls=%async_computation | async-start | bytes 14680064 | tf_op jit(solution)/shard_map/all_to_all | solution.py:308
  491.0 103.2 %all-to-all-start.1 = ((bf16[8,128,3584]{2,1,0:T(8,128)(2,1)}), bf16[8,128,3584]{2,1,0:T(8,128)(2,1)}, u32[]{:S(2)}, u32[]{:S(2)}) async-start(bf16[8,128,3584]{2,1,0:T(8,128)(2,1)} %add_convert_fusion), calls=%async_computation.1 | async-start | bytes 14680064 | tf_op jit(solution)/shard_map/all_to_all | solution.py:308
  594.1 10.5 %copy-start = (f32[256,3584]{1,0:T(8,128)S(1)}, f32[256,3584]{1,0:T(8,128)}, u32[]{:S(2)}) copy-start(f32[256,3584]{1,0:T(8,128)} %shared.3) | copy-start | bytes 11010052
Sparse Core Ops, SparseCore 0:
  9.6 72.7 all-gather.2
  84.6 69.5 all-gather.4

commit v2 on v1

--- a/solution.py
+++ b/solution.py
@@ -26,53 +26,111 @@
 FB = 512
 NB = FF // FB
 SB = 512
-SA_BLOCKS = 19
+SA_BLOCKS = 8
 VMEM = 64 * 1024 * 1024 - 65536
 
 
-def shared_kernel(x_ref, wg_ref, wu_ref, wd_ref, acc_in, acc_ref, *, first):
+def shared_kernel(start_ref, x_ref, wg_ref, wu_ref, wd_ref, acc_in, *rest, last):
     j = pl.program_id(0)
+    acc_ref = rest[-1]
 
     @pl.when(j == 0)
     def _():
-        if first:
+        if last:
+            acc_ref[...] = acc_in[...]
+        else:
             acc_ref[...] = jnp.zeros_like(acc_ref)
-        else:
-            acc_ref[...] = acc_in[...]
 
     x = x_ref[...]
     g = jnp.dot(x, wg_ref[...], preferred_element_type=jnp.float32)
     u = jnp.dot(x, wu_ref[...], preferred_element_type=jnp.float32)
     h = (jax.nn.silu(g) * u).astype(jnp.bfloat16)
     acc_ref[...] += jnp.dot(h, wd_ref[...], preferred_element_type=jnp.float32)
+    if last:
+        own_ref, other_ref = rest[:2]
+
+        @pl.when(j == pl.num_programs(0) - 1)
+        def _():
+            own_ref[...] = acc_ref[:TOK, :]
+            other_ref[...] = acc_ref[TOK:, :].astype(jnp.bfloat16)
 
 
 def shared(x, wg, wu, wd, start, count, acc=None):
-    first = acc is None
-    rows = x.shape[0]
-    if first:
+    rows = 2 * TOK
+    last = acc is not None
+    whole = pl.BlockSpec((rows, D), lambda j, s: (0, 0))
+    if last:
+        acc_spec = whole
+        out_specs = [pl.BlockSpec((TOK, D), lambda j, s: (0, 0))] * 2
+        out_shape = [jax.ShapeDtypeStruct((TOK, D), jnp.float32), jax.ShapeDtypeStruct((TOK, D), jnp.bfloat16)]
+        scratch = [pltpu.VMEM((rows, D), jnp.float32)]
+    else:
         acc = jnp.zeros((8, 128), jnp.float32)
-        acc_spec = pl.BlockSpec((8, 128), lambda j: (0, 0))
-    else:
-        acc_spec = pl.BlockSpec((rows, D), lambda j: (0, 0))
+        acc_spec = pl.BlockSpec((8, 128), lambda j, s: (0, 0))
+        out_specs, out_shape, scratch = whole, jax.ShapeDtypeStruct((rows, D), jnp.float32), []
     return pl.pallas_call(
-        functools.partial(shared_kernel, first=first),
-        grid=(count,),
-        in_specs=[
-            pl.BlockSpec((rows, D), lambda j: (0, 0)),
-            pl.BlockSpec((D, SB), lambda j: (0, start + j)),
-            pl.BlockSpec((D, SB), lambda j: (0, start + j)),
-            pl.BlockSpec((SB, D), lambda j: (start + j, 0)),
-            acc_spec,
-        ],
-        out_specs=pl.BlockSpec((rows, D), lambda j: (0, 0)),
-        out_shape=jax.ShapeDtypeStruct((rows, D), jnp.float32),
+        functools.partial(shared_kernel, last=last),
+        grid_spec=pltpu.PrefetchScalarGridSpec(
+            num_scalar_prefetch=1,
+            grid=(count,),
+            in_specs=[
+                whole,
+                pl.BlockSpec((D, SB), lambda j, s: (0, s[0] + j)),
+                pl.BlockSpec((D, SB), lambda j, s: (0, s[0] + j)),
+                pl.BlockSpec((SB, D), lambda j, s: (s[0] + j, 0)),
+                acc_spec,
+            ],
+            out_specs=out_specs,
+            scratch_shapes=scratch,
+        ),
+        out_shape=out_shape,
         compiler_params=pltpu.CompilerParams(vmem_limit_bytes=VMEM),
         cost_estimate=pl.CostEstimate(
             flops=6 * rows * D * SB * count, bytes_accessed=6 * D * SB * count, transcendentals=rows * SB * count
         ),
         name="shared",
-    )(x, wg, wu, wd, acc)
+    )(start, x, wg, wu, wd, acc)
+
+
+def final_kernel(chip_ref, own_ref, other_ref, *rest):
+    y_ref = rest[-1]
+    chip = chip_ref[0]
+    sums = []
+    for c in range(CHUNKS):
+        back_ref, keep_ref, got_ref = rest[3 * c : 3 * c + 3]
+        t = keep_ref[0] + got_ref[0].astype(jnp.float32)
+        for k in range(CHIPS):
+            t += jnp.where(chip == k, 0.0, back_ref[k].astype(jnp.float32))
+        sums.append(t)
+    pieces = []
+    for g in range(16 // GROUP):
+        for c in range(CHUNKS):
+            pieces.append(sums[c][g * GROUP : (g + 1) * GROUP])
+    t = jnp.concatenate(pieces, axis=0)
+    y_ref[...] = (t + (own_ref[...] + other_ref[...].astype(jnp.float32))).astype(jnp.bfloat16)
+
+
+def final(chip, own, other, parts):
+    rows = 16 * CHUNKS
+    specs = [pl.BlockSpec((rows, D), lambda i, c: (i, 0))] * 2
+    args = [own, other]
+    for back, keep, got in parts:
+        specs.append(pl.BlockSpec((CHIPS, 16, D), lambda i, c: (0, i, 0)))
+        specs += [pl.BlockSpec((1, 16, D), lambda i, c: (c[0], i, 0))] * 2
+        args += [back, keep, got]
+    return pl.pallas_call(
+        final_kernel,
+        grid_spec=pltpu.PrefetchScalarGridSpec(
+            num_scalar_prefetch=1,
+            grid=(TOK // rows,),
+            in_specs=specs,
+            out_specs=pl.BlockSpec((rows, D), lambda i, c: (i, 0)),
+        ),
+        out_shape=jax.ShapeDtypeStruct((TOK, D), jnp.bfloat16),
+        compiler_params=pltpu.CompilerParams(vmem_limit_bytes=40 * 1024 * 1024),
+        cost_estimate=pl.CostEstimate(flops=20 * TOK * D, bytes_accessed=24 * CHIPS * TOK * D, transcendentals=0),
+        name="final",
+    )(chip, *args)
 
 
 def routed_kernel(
@@ -103,11 +161,13 @@
             fetch(a, slot).wait()
             m = meta_ref[a]
             rows = lax.broadcasted_iota(jnp.int32, (WIN, CT), 0).astype(jnp.float32)
+            pick = [jnp.where(m[q : q + 1, :] == rows, 1.0, 0.0) for q in range(2)]
+            pick = jnp.concatenate(pick, axis=0).astype(jnp.bfloat16)
+            both = jnp.dot(pick, xbuf[slot], preferred_element_type=jnp.float32)
+            row = lax.broadcasted_iota(jnp.int32, (16, 1), 0)
             for q in range(2):
-                pick = jnp.where(m[q : q + 1, :] == rows, 1.0, 0.0).astype(jnp.bfloat16)
-                new = jnp.dot(pick, xbuf[slot], preferred_element_type=jnp.float32)
+                new = both[q * WIN : (q + 1) * WIN]
                 base = pl.multiple_of(base_ref[q, a], 16)
-                row = lax.broadcasted_iota(jnp.int32, (16, 1), 0)
                 old = zbuf[q, pl.ds(base, 16), :].astype(jnp.float32)
                 zbuf[q, pl.ds(base, 16), :] = jnp.where(row < off_ref[q, a], old, new[:16]).astype(jnp.bfloat16)
                 zbuf[q, pl.ds(base + 16, WIN - 16), :] = new[16:].astype(jnp.bfloat16)
@@ -283,10 +343,13 @@
         gathered = [
             lax.all_gather(xs[:, c].reshape(CT, D), "ep", axis=0) for c in range(CHUNKS)
         ]
-        acc = shared(x, s_gate, s_up, s_down, 0, SA_BLOCKS)
-        parts = []
         pair = [(i, i ^ 1) for i in range(NDEV)]
         groups = [[2 * k + c for k in range(CHIPS)] for c in range(2)]
+        each = SFF // SB // 2
+        both = jnp.concatenate([x, lax.ppermute(x, "ep", pair)], axis=0)
+        start = (core * each)[None]
+        acc = shared(both, s_gate, s_up, s_down, start, SA_BLOCKS)
+        parts = []
         after = acc
         for c in range(CHUNKS):
             base, off, tiles, meta = plan[c]
@@ -294,29 +357,19 @@
             if c == 0:
                 acc = after
             else:
-                parts[-1] = (parts[-1][0], after)
+                parts[-1] = (after, *parts[-1][1:])
             keep, away = routed(base, off, tiles, core[None], tokens, meta, w_gate, w_up, w_down)
             got = lax.ppermute(away, "ep", pair)
-            total = (keep + got.astype(jnp.float32)).astype(jnp.bfloat16)
-            own = lax.dynamic_index_in_dim(keep, chip, 0, keepdims=False)
-            own = own + lax.dynamic_index_in_dim(got, chip, 0, keepdims=False).astype(jnp.float32)
-            parts.append((own, total))
-            after = total
-        x, acc, last = lax.optimization_barrier((x, acc, after))
-        parts[-1] = (parts[-1][0], last)
+            after = (keep + got.astype(jnp.float32)).astype(jnp.bfloat16)
+            parts.append((after, keep, got))
+        both, acc, after = lax.optimization_barrier((both, acc, after))
+        parts[-1] = (after, *parts[-1][1:])
         for c in range(CHUNKS):
-            back = lax.all_to_all(parts[c][1], "ep", 0, 0, axis_index_groups=groups, tiled=True)
-            parts[c] = (parts[c][0], back)
-        rest = shared(x, s_gate, s_up, s_down, SA_BLOCKS, SFF // SB - SA_BLOCKS, acc)
-        rest = rest.reshape(TOK // (GROUP * CHUNKS), CHUNKS, GROUP, D)
-        outs = []
-        others = (jnp.arange(CHIPS) != chip)[:, None, None]
-        for c in range(CHUNKS):
-            own, back = parts[c]
-            t = own + jnp.sum(jnp.where(others, back.astype(jnp.float32), 0.0), axis=0)
-            outs.append(t.reshape(TOK // (GROUP * CHUNKS), GROUP, D) + rest[:, c])
-        y = jnp.stack(outs, axis=1).reshape(TOK, D).astype(jnp.bfloat16)
-        return y[None, None]
+            back = lax.all_to_all(parts[c][0], "ep", 0, 0, axis_index_groups=groups, tiled=True)
+            parts[c] = (back, *parts[c][1:])
+        own, other = shared(both, s_gate, s_up, s_down, start + SA_BLOCKS, each - SA_BLOCKS, acc)
+        other = lax.ppermute(other, "ep", pair)
+        return final(chip[None], own, other, parts)[None, None]
 
     row = P("dp", "ep", None, None)
     return jax.shard_map(

time: 619 us -> 594 us (0.960)
  Pallas kernels: 411 us -> 394 us
  other arithmetic: 39.4 us -> 26.1 us
    pallas_call x2 -> x3, Pallas kernels: 167 us -> 150 us  [the longest x2 140 us: shared(): pl.pallas_call(functools.partial(shared_kernel, last=last), grid_spec=plt...]
    reduce_sum x1 -> x0, other arithmetic: 10.5 us -> none  [layer(): t = own + jnp.sum(jnp.where(others, back.astype(jnp.float32), 0.0), axis=0)]
    another operation x2 -> x0, other arithmetic: 6.43 us -> none
  transfers between devices with their start and end apart: 6 -> 8, of which waited for: 4 -> 5; matrix products, arithmetic and copies ran while one was open for 4% -> 5% of each run, Pallas kernels for 46% -> 44%
where the time goes in v2:
time: 594 us; the launch traced here: 593 us
  Pallas kernels  394 us (66%)
  waiting for transfers between devices  117 us (20%)
  other arithmetic  26.1 us (4%)
  starting transfers between devices  15.6 us (3%)
  blocking collectives  14.8 us (2%)
  between operations  13.5 us (2%)
  local copies, waits for them, and re-layouts  11.5 us (2%)
    pallas_call x2, Pallas kernels, routed(): pl.pallas_call(routed_kernel, grid_spec=grid_spec, out_shape=[jax.ShapeDt...  244 us
    pallas_call x2, Pallas kernels, shared(): pl.pallas_call(functools.partial(shared_kernel, last=last), grid_spec=plt...  140 us
    all_to_all x2, waiting for transfers between devices, layer(): lax.all_to_all(parts[c][0], 'ep', 0, 0, axis_index_groups=groups, tiled=T...  98.3 us
    convert_element_type x2, other arithmetic, layer(): after = (keep + got.astype(jnp.float32)).astype(jnp.bfloat16)  19 us
    all_gather x1, blocking collectives, layer(): lax.all_gather(packed, 'ep', axis=0).reshape(NDEV, 2 * TOP, CHUNKS, CT)  14.8 us
    all_to_all x2, starting transfers between devices, layer(): lax.all_to_all(parts[c][0], 'ep', 0, 0, axis_index_groups=groups, tiled=T...  14.7 us
    ppermute x2, waiting for transfers between devices, layer(): got = lax.ppermute(away, 'ep', pair)  14.2 us
  transfers between devices with their start and end apart: 8, of which 5 were waited for; matrix products, arithmetic and copies ran while one was open for 5% of the time, Pallas kernels for 44%

profile of v2, /device:TPU:0, one launch (start us, length us, event | category | flops | bytes accessed | tf_op | source)
XLA Modules:
  0.0 593.0 jit_solution(16602384958981243793)
XLA Ops:
  6.5 3.0 slice_bitcast_fusion
  9.6 0.7 all-gather.5.cloned.1.call-update
  10.3 0.8 collective-permute-start
  11.0 0.7 convert_element_type.64
  11.9 0.7 select_convert_fusion
  12.7 0.2 maximum_bitcast_fusion
  12.9 0.2 copy.73
  13.2 14.8 %all_gather.10 = bf16[16,16,256]{2,1,0:T(8,128)(2,1)S(1)} all-gather(bf16[1,16,256]{2,1,0:T(8,128)(2,1)S(1)} %copy.74), channel_id=1, replica_groups=mesh['dp'=1,'ep'=16] {'ep'}, dimensions={0}, use_global_device_ids=true | all-gather | bytes 139264 | tf_op jit(solution)/shard_map/all_gather | solution.py:339
  28.2 0.4 convert_reduce_fusion
  28.9 0.7 slice_reduce_fusion
  29.8 0.6 fusion.16
  30.4 0.6 fusion.17
  31.0 0.1 fusion.3
  31.2 0.7 maximum_maximum_fusion.1
  32.0 4.1 pad_maximum_fusion.x_ref
  36.1 0.6 broadcast_in_dim.49.acc_in
  36.7 57.1 %shared.2.acc_in = f32[512,3584]{1,0:T(8,128)} custom-call(s32[1]{0:T(128)} %bitcast.1.start_ref, bf16[512,3584]{1,0:T(8,128)(2,1)} %pad_maximum_fusion.x_ref, bf16[3584,20480]{1,0:T(8,128)(2,1)} %wg_ref.7, bf16[3584,20480]{1,0:T(8,128)(2,1)} %wu_ref.7, bf16[20480,3584]{1,0:T(8,128)(2,1)} %wd_ref.7, f32[8,128]{1,0:T(8,128)} %broadcast_in_dim.49.acc_in), custom_call_target="tpu_custom_call" | custom-call | flops 45097156608 | bytes 88080384 | tf_op jit(solution)/shard_map/shared/pallas_call | solution.py:71
  93.8 118.5 %routed.2 = (f32[8,128,3584]{2,1,0:T(8,128)}, bf16[8,128,3584]{2,1,0:T(8,128)(2,1)}) custom-call(s32[2,16]{1,0:T(2,128)} %bitcast.66, s32[2,16]{1,0:T(2,128)} %bitcast.65, s32[2]{0:T(128)} %get-tuple-element.34.tiles_ref, s32[1]{0:T(128)} %bitcast.12.core_ref, bf16[16,128,3584]{2,1,0:T(8,128)(2,1)} %all-gather.3.cloned.1.call-done.x_hbm, ...), custom_call_target="tpu_custom_call" | custom-call | flops 70464307200 | bytes 110100480 | tf_op jit(solution)/shard_map/routed/pallas_call | solution.py:288
  212.3 11.9 %collective-permute-done.1.rest_2_ = bf16[8,128,3584]{2,1,0:T(8,128)(2,1)S(1)} collective-permute-done((bf16[8,128,3584]{2,1,0:T(8,128)(2,1)}, bf16[8,128,3584]{2,1,0:T(8,128)(2,1)S(1)}, u32[]{:S(2)}, u32[]{:S(2)}) %collective-permute-start.1) | collective-permute-done | bytes 7340064 | tf_op jit(solution)/shard_map/ppermute | solution.py:362
  224.2 2.9 copy-done.1
  227.1 8.5 %add_convert_fusion.1 = bf16[8,128,3584]{2,1,0:T(8,128)(2,1)} fusion(f32[8,128,3584]{2,1,0:T(8,128)} %get-tuple-element.20.rest_1_, bf16[8,128,3584]{2,1,0:T(8,128)(2,1)S(1)} %collective-permute-done.1.rest_2_), kind=kLoop, calls=%fused_computation.1 | loop fusion | flops 11010048 | bytes 29360128 | tf_op jit(solution)/shard_map/convert_element_type | solution.py:363
  235.6 125.2 %routed.3 = (f32[8,128,3584]{2,1,0:T(8,128)}, bf16[8,128,3584]{2,1,0:T(8,128)(2,1)}) custom-call(s32[2,16]{1,0:T(2,128)} %bitcast.64, s32[2,16]{1,0:T(2,128)} %bitcast.63, s32[2]{0:T(128)} %get-tuple-element.35.tiles_ref, s32[1]{0:T(128)} %bitcast.12.core_ref, bf16[16,128,3584]{2,1,0:T(8,128)(2,1)} %all-gather.5.cloned.1.call-done.x_hbm, ...), custom_call_target="tpu_custom_call" | custom-call | flops 70464307200 | bytes 110100480 | tf_op jit(solution)/shard_map/routed/pallas_call | solution.py:288
  360.9 9.6 %all-to-all-start = ((bf16[8,128,3584]{2,1,0:T(8,128)(2,1)}), bf16[8,128,3584]{2,1,0:T(8,128)(2,1)}, u32[]{:S(2)}, u32[]{:S(2)}) async-start(bf16[8,128,3584]{2,1,0:T(8,128)(2,1)} %add_convert_fusion.1), calls=%async_computation | async-start | bytes 14680064 | tf_op jit(solution)/shard_map/all_to_all | solution.py:368
  370.5 2.4 collective-permute-done.2.rest_5_
  372.9 10.5 %add_convert_fusion = bf16[8,128,3584]{2,1,0:T(8,128)(2,1)} fusion(f32[8,128,3584]{2,1,0:T(8,128)} %get-tuple-element.23.rest_4_, bf16[8,128,3584]{2,1,0:T(8,128)(2,1)} %collective-permute-done.2.rest_5_), kind=kLoop, calls=%fused_computation | loop fusion | flops 11010048 | bytes 29360128 | tf_op jit(solution)/shard_map/convert_element_type | solution.py:363
  383.4 87.0 %all-to-all-done.rest_0_ = bf16[8,128,3584]{2,1,0:T(8,128)(2,1)} async-done(((bf16[8,128,3584]{2,1,0:T(8,128)(2,1)}), bf16[8,128,3584]{2,1,0:T(8,128)(2,1)}, u32[]{:S(2)}, u32[]{:S(2)}) %all-to-all-start) | async-done | bytes 7340064 | tf_op jit(solution)/shard_map/all_to_all | solution.py:368
  470.4 5.1 all-to-all-start.1
  475.5 82.7 %shared.3 = (f32[256,3584]{1,0:T(8,128)}, bf16[256,3584]{1,0:T(8,128)(2,1)}) custom-call(s32[1]{0:T(128)S(6)} %add.35.start_ref, bf16[512,3584]{1,0:T(8,128)(2,1)} %pad_maximum_fusion.x_ref, bf16[3584,20480]{1,0:T(8,128)(2,1)} %wg_ref.7, bf16[3584,20480]{1,0:T(8,128)(2,1)} %wu_ref.7, bf16[20480,3584]{1,0:T(8,128)(2,1)} %wd_ref.7, f32[512,3584]{1,0:T(8,128)} %shared.2.acc_in), custom_call_target="tpu_custom_call" | custom-call | flops 67645734912 | bytes 132120576 | tf_op jit(solution)/shard_map/shared/pallas_call | solution.py:71
  558.2 4.0 collective-permute-done.3.other_ref
  562.2 11.3 %all-to-all-done.1.rest_3_ = bf16[8,128,3584]{2,1,0:T(8,128)(2,1)} async-done(((bf16[8,128,3584]{2,1,0:T(8,128)(2,1)}), bf16[8,128,3584]{2,1,0:T(8,128)(2,1)}, u32[]{:S(2)}, u32[]{:S(2)}) %all-to-all-start.1) | async-done | bytes 7340064 | tf_op jit(solution)/shard_map/all_to_all | solution.py:368
  573.5 2.0 copy-done
  575.6 10.7 %final.1 = bf16[256,3584]{1,0:T(8,128)(2,1)} custom-call(s32[1]{0:T(128)} %bitcast.chip_ref, f32[256,3584]{1,0:T(8,128)S(1)} %copy-done, bf16[256,3584]{1,0:T(8,128)(2,1)S(1)} %collective-permute-done.3.other_ref, bf16[8,128,3584]{2,1,0:T(8,128)(2,1)} %all-to-all-done.rest_0_, f32[8,128,3584]{2,1,0:T(8,128)} %get-tuple-element.20.rest_1_, ...), custom_call_target="tpu_custom_call" | custom-call | flops 18350080 | bytes 176160768 | tf_op jit(solution)/shard_map/final/pallas_call | solution.py:121
  (35 shorter events, 1.3 us)
Async XLA Ops:
  6.5 25.4 %copy-start.2 = (bf16[1,1,256,3584]{3,2,1,0:T(8,128)(2,1)S(1)}, bf16[1,1,256,3584]{3,2,1,0:T(8,128)(2,1)}, u32[]{:S(2)}) copy-start(bf16[1,1,256,3584]{3,2,1,0:T(8,128)(2,1)} %param.10) | copy-start | bytes 5505028
  6.5 87.2 %all-gather.3.cloned.1.call-start = ((), (), s32[]{:S(2)}) async-start(), calls=%async_computation.2 | async-start | bytes 15597568 | tf_op jit(solution)/shard_map/all_gather | solution.py:344
  9.5 226.1 %all-gather.5.cloned.1.call-start = ((), (), s32[]{:S(2)}) async-start(), calls=%async_computation.3 | async-start | bytes 15597568 | tf_op jit(solution)/shard_map/all_gather | solution.py:344
  10.3 21.7 %collective-permute-start = (bf16[256,3584]{1,0:T(8,128)(2,1)}, bf16[256,3584]{1,0:T(8,128)(2,1)}, u32[]{:S(2)}, u32[]{:S(2)}) collective-permute-start(bf16[256,3584]{1,0:T(8,128)(2,1)} %bitcast.58), channel_id=1, source_target_pairs={{0,1},{1,0},{2,3},{3,2},{4,5},{5,4},{6,7},{7,6},{8,9},{9,8},{10,11... | collective-permute-start | bytes 5505032 | tf_op jit(solution)/shard_map/ppermute | solution.py:349
  212.3 11.9 %collective-permute-start.1 = (bf16[8,128,3584]{2,1,0:T(8,128)(2,1)}, bf16[8,128,3584]{2,1,0:T(8,128)(2,1)S(1)}, u32[]{:S(2)}, u32[]{:S(2)}) collective-permute-start(bf16[8,128,3584]{2,1,0:T(8,128)(2,1)} %get-tuple-element.21), channel_id=1, source_target_pairs={{0,1},{1,0},{2,3},{3,2},{4,5},{5,4},{6,7},{7,6},{8,9},{9,8},{10,11... | collective-permute-start | bytes 22020104 | tf_op jit(solution)/shard_map/ppermute | solution.py:362
  224.2 2.9 copy-start.1
  360.8 12.0 %collective-permute-start.2 = (bf16[8,128,3584]{2,1,0:T(8,128)(2,1)}, bf16[8,128,3584]{2,1,0:T(8,128)(2,1)}, u32[]{:S(2)}, u32[]{:S(2)}) collective-permute-start(bf16[8,128,3584]{2,1,0:T(8,128)(2,1)} %get-tuple-element.24), channel_id=1, source_target_pairs={{0,1},{1,0},{2,3},{3,2},{4,5},{5,4},{6,7},{7,6},{8,9},{9,8},{10,11... | collective-permute-start | bytes 22020104 | tf_op jit(solution)/shard_map/ppermute | solution.py:362
  360.9 109.5 %all-to-all-start = ((bf16[8,128,3584]{2,1,0:T(8,128)(2,1)}), bf16[8,128,3584]{2,1,0:T(8,128)(2,1)}, u32[]{:S(2)}, u32[]{:S(2)}) async-start(bf16[8,128,3584]{2,1,0:T(8,128)(2,1)} %add_convert_fusion.1), calls=%async_computation | async-start | bytes 14680064 | tf_op jit(solution)/shard_map/all_to_all | solution.py:368
  470.4 103.1 %all-to-all-start.1 = ((bf16[8,128,3584]{2,1,0:T(8,128)(2,1)}), bf16[8,128,3584]{2,1,0:T(8,128)(2,1)}, u32[]{:S(2)}, u32[]{:S(2)}) async-start(bf16[8,128,3584]{2,1,0:T(8,128)(2,1)} %add_convert_fusion), calls=%async_computation.1 | async-start | bytes 14680064 | tf_op jit(solution)/shard_map/all_to_all | solution.py:368
  558.2 4.0 collective-permute-start.3
  573.5 2.0 copy-start
Sparse Core Ops, SparseCore 0:
  9.6 72.7 all-gather.2
  84.7 69.5 all-gather.4

commit v3 on v2

--- a/solution.py
+++ b/solution.py
@@ -26,7 +26,7 @@
 FB = 512
 NB = FF // FB
 SB = 512
-SA_BLOCKS = 8
+SA_BLOCKS = 6
 VMEM = 64 * 1024 * 1024 - 65536
 
 
@@ -149,7 +149,9 @@
     @pl.when((e == 0) & (p == 0) & (j == 0))
     def _():
         fetch(0, 0).start()
-        zbuf[...] = jnp.zeros_like(zbuf)
+        for q in range(2):
+            tail = jnp.minimum(base_ref[q, NDEV - 1] + WIN, ZROWS - 128)
+            zbuf[q, pl.ds(pl.multiple_of(tail, 16), 128), :] = jnp.zeros((128, D), jnp.bfloat16)
 
         def step(a, c):
             slot = lax.rem(a, 2)

time: 594 us -> 583 us (0.981)
  waiting for transfers between devices: 117 us -> 106 us
    all_to_all x2, waiting for transfers between devices: 98.3 us -> 87.1 us  [layer(): lax.all_to_all(parts[c][0], 'ep', 0, 0, axis_index_groups=groups, tiled=T...]
where the time goes in v3:
time: 583 us; the launch traced here: 582 us
  Pallas kernels  394 us (68%)
  waiting for transfers between devices  106 us (18%)
  other arithmetic  26.1 us (4%)
  starting transfers between devices  16 us (3%)
  blocking collectives  14.8 us (3%)
  between operations  13.5 us (2%)
  local copies, waits for them, and re-layouts  11.5 us (2%)
    pallas_call x2, Pallas kernels, routed(): pl.pallas_call(routed_kernel, grid_spec=grid_spec, out_shape=[jax.ShapeDt...  244 us
    pallas_call x2, Pallas kernels, shared(): pl.pallas_call(functools.partial(shared_kernel, last=last), grid_spec=plt...  140 us
    all_to_all x2, waiting for transfers between devices, layer(): lax.all_to_all(parts[c][0], 'ep', 0, 0, axis_index_groups=groups, tiled=T...  87.1 us
    convert_element_type x2, other arithmetic, layer(): after = (keep + got.astype(jnp.float32)).astype(jnp.bfloat16)  19 us
    all_to_all x2, starting transfers between devices, layer(): lax.all_to_all(parts[c][0], 'ep', 0, 0, axis_index_groups=groups, tiled=T...  14.8 us
    all_gather x1, blocking collectives, layer(): lax.all_gather(packed, 'ep', axis=0).reshape(NDEV, 2 * TOP, CHUNKS, CT)  14.8 us
    ppermute x2, waiting for transfers between devices, layer(): got = lax.ppermute(away, 'ep', pair)  14.1 us
  transfers between devices with their start and end apart: 8, of which 5 were waited for; matrix products, arithmetic and copies ran while one was open for 5% of the time, Pallas kernels for 44%

profile of v3, /device:TPU:0, one launch (start us, length us, event | category | flops | bytes accessed | tf_op | source)
XLA Modules:
  0.0 582.0 jit_solution(14405743609260789656)
XLA Ops:
  6.5 3.0 slice_bitcast_fusion
  9.6 0.7 all-gather.5.cloned.1.call-update
  10.3 0.8 collective-permute-start
  11.0 0.7 convert_element_type.64
  11.9 0.7 select_convert_fusion
  12.7 0.2 maximum_bitcast_fusion
  12.9 0.2 copy.73
  13.2 14.8 %all_gather.10 = bf16[16,16,256]{2,1,0:T(8,128)(2,1)S(1)} all-gather(bf16[1,16,256]{2,1,0:T(8,128)(2,1)S(1)} %copy.74), channel_id=1, replica_groups=mesh['dp'=1,'ep'=16] {'ep'}, dimensions={0}, use_global_device_ids=true | all-gather | bytes 139264 | tf_op jit(solution)/shard_map/all_gather | solution.py:341
  28.2 0.4 convert_reduce_fusion
  28.9 0.7 slice_reduce_fusion
  29.8 0.6 fusion.16
  30.4 0.6 fusion.17
  31.2 0.7 maximum_maximum_fusion.1
  32.0 4.1 pad_maximum_fusion.x_ref
  36.1 0.6 broadcast_in_dim.49.acc_in
  36.7 45.3 %shared.2.acc_in = f32[512,3584]{1,0:T(8,128)} custom-call(s32[1]{0:T(128)} %bitcast.1.start_ref, bf16[512,3584]{1,0:T(8,128)(2,1)} %pad_maximum_fusion.x_ref, bf16[3584,20480]{1,0:T(8,128)(2,1)} %wg_ref.7, bf16[3584,20480]{1,0:T(8,128)(2,1)} %wu_ref.7, bf16[20480,3584]{1,0:T(8,128)(2,1)} %wd_ref.7, f32[8,128]{1,0:T(8,128)} %broadcast_in_dim.49.acc_in), custom_call_target="tpu_custom_call" | custom-call | flops 33822867456 | bytes 66060288 | tf_op jit(solution)/shard_map/shared/pallas_call | solution.py:71
  82.0 0.5 all-gather.3.cloned.1.call-done.x_hbm
  82.4 118.5 %routed.2 = (f32[8,128,3584]{2,1,0:T(8,128)}, bf16[8,128,3584]{2,1,0:T(8,128)(2,1)}) custom-call(s32[2,16]{1,0:T(2,128)} %bitcast.66, s32[2,16]{1,0:T(2,128)} %bitcast.65, s32[2]{0:T(128)} %get-tuple-element.34.tiles_ref, s32[1]{0:T(128)} %bitcast.12.core_ref, bf16[16,128,3584]{2,1,0:T(8,128)(2,1)} %all-gather.3.cloned.1.call-done.x_hbm, ...), custom_call_target="tpu_custom_call" | custom-call | flops 70464307200 | bytes 110100480 | tf_op jit(solution)/shard_map/routed/pallas_call | solution.py:290
  201.0 11.9 %collective-permute-done.1.rest_2_ = bf16[8,128,3584]{2,1,0:T(8,128)(2,1)S(1)} collective-permute-done((bf16[8,128,3584]{2,1,0:T(8,128)(2,1)}, bf16[8,128,3584]{2,1,0:T(8,128)(2,1)S(1)}, u32[]{:S(2)}, u32[]{:S(2)}) %collective-permute-start.1) | collective-permute-done | bytes 7340064 | tf_op jit(solution)/shard_map/ppermute | solution.py:364
  212.9 2.9 copy-done.1
  215.8 8.5 %add_convert_fusion.1 = bf16[8,128,3584]{2,1,0:T(8,128)(2,1)} fusion(f32[8,128,3584]{2,1,0:T(8,128)} %get-tuple-element.20.rest_1_, bf16[8,128,3584]{2,1,0:T(8,128)(2,1)S(1)} %collective-permute-done.1.rest_2_), kind=kLoop, calls=%fused_computation.1 | loop fusion | flops 11010048 | bytes 29360128 | tf_op jit(solution)/shard_map/convert_element_type | solution.py:365
  224.3 125.0 %routed.3 = (f32[8,128,3584]{2,1,0:T(8,128)}, bf16[8,128,3584]{2,1,0:T(8,128)(2,1)}) custom-call(s32[2,16]{1,0:T(2,128)} %bitcast.64, s32[2,16]{1,0:T(2,128)} %bitcast.63, s32[2]{0:T(128)} %get-tuple-element.35.tiles_ref, s32[1]{0:T(128)} %bitcast.12.core_ref, bf16[16,128,3584]{2,1,0:T(8,128)(2,1)} %all-gather.5.cloned.1.call-done.x_hbm, ...), custom_call_target="tpu_custom_call" | custom-call | flops 70464307200 | bytes 110100480 | tf_op jit(solution)/shard_map/routed/pallas_call | solution.py:290
  349.4 9.7 %all-to-all-start = ((bf16[8,128,3584]{2,1,0:T(8,128)(2,1)}), bf16[8,128,3584]{2,1,0:T(8,128)(2,1)}, u32[]{:S(2)}, u32[]{:S(2)}) async-start(bf16[8,128,3584]{2,1,0:T(8,128)(2,1)} %add_convert_fusion.1), calls=%async_computation | async-start | bytes 14680064 | tf_op jit(solution)/shard_map/all_to_all | solution.py:370
  359.1 2.2 collective-permute-done.2.rest_5_
  361.4 10.5 %add_convert_fusion = bf16[8,128,3584]{2,1,0:T(8,128)(2,1)} fusion(f32[8,128,3584]{2,1,0:T(8,128)} %get-tuple-element.23.rest_4_, bf16[8,128,3584]{2,1,0:T(8,128)(2,1)} %collective-permute-done.2.rest_5_), kind=kLoop, calls=%fused_computation | loop fusion | flops 11010048 | bytes 29360128 | tf_op jit(solution)/shard_map/convert_element_type | solution.py:365
  371.9 87.1 %all-to-all-done.rest_0_ = bf16[8,128,3584]{2,1,0:T(8,128)(2,1)} async-done(((bf16[8,128,3584]{2,1,0:T(8,128)(2,1)}), bf16[8,128,3584]{2,1,0:T(8,128)(2,1)}, u32[]{:S(2)}, u32[]{:S(2)}) %all-to-all-start) | async-done | bytes 7340064 | tf_op jit(solution)/shard_map/all_to_all | solution.py:370
  459.0 5.1 all-to-all-start.1
  464.1 94.3 %shared.3 = (f32[256,3584]{1,0:T(8,128)}, bf16[256,3584]{1,0:T(8,128)(2,1)}) custom-call(s32[1]{0:T(128)S(6)} %add.35.start_ref, bf16[512,3584]{1,0:T(8,128)(2,1)} %pad_maximum_fusion.x_ref, bf16[3584,20480]{1,0:T(8,128)(2,1)} %wg_ref.7, bf16[3584,20480]{1,0:T(8,128)(2,1)} %wu_ref.7, bf16[20480,3584]{1,0:T(8,128)(2,1)} %wd_ref.7, f32[512,3584]{1,0:T(8,128)} %shared.2.acc_in), custom_call_target="tpu_custom_call" | custom-call | flops 78920024064 | bytes 154140672 | tf_op jit(solution)/shard_map/shared/pallas_call | solution.py:71
  558.5 0.3 collective-permute-start.3
  558.8 3.7 collective-permute-done.3.other_ref
  562.5 2.0 copy-done
  564.5 10.7 %final.1 = bf16[256,3584]{1,0:T(8,128)(2,1)} custom-call(s32[1]{0:T(128)} %bitcast.chip_ref, f32[256,3584]{1,0:T(8,128)S(1)} %copy-done, bf16[256,3584]{1,0:T(8,128)(2,1)S(1)} %collective-permute-done.3.other_ref, bf16[8,128,3584]{2,1,0:T(8,128)(2,1)} %all-to-all-done.rest_0_, f32[8,128,3584]{2,1,0:T(8,128)} %get-tuple-element.20.rest_1_, ...), custom_call_target="tpu_custom_call" | custom-call | flops 18350080 | bytes 176160768 | tf_op jit(solution)/shard_map/final/pallas_call | solution.py:121
  (35 shorter events, 1.4 us)
Async XLA Ops:
  6.5 25.4 %copy-start.2 = (bf16[1,1,256,3584]{3,2,1,0:T(8,128)(2,1)S(1)}, bf16[1,1,256,3584]{3,2,1,0:T(8,128)(2,1)}, u32[]{:S(2)}) copy-start(bf16[1,1,256,3584]{3,2,1,0:T(8,128)(2,1)} %param.10) | copy-start | bytes 5505028
  6.5 75.9 %all-gather.3.cloned.1.call-start = ((), (), s32[]{:S(2)}) async-start(), calls=%async_computation.2 | async-start | bytes 15597568 | tf_op jit(solution)/shard_map/all_gather | solution.py:346
  9.5 214.8 %all-gather.5.cloned.1.call-start = ((), (), s32[]{:S(2)}) async-start(), calls=%async_computation.3 | async-start | bytes 15597568 | tf_op jit(solution)/shard_map/all_gather | solution.py:346
  10.3 21.7 %collective-permute-start = (bf16[256,3584]{1,0:T(8,128)(2,1)}, bf16[256,3584]{1,0:T(8,128)(2,1)}, u32[]{:S(2)}, u32[]{:S(2)}) collective-permute-start(bf16[256,3584]{1,0:T(8,128)(2,1)} %bitcast.58), channel_id=1, source_target_pairs={{0,1},{1,0},{2,3},{3,2},{4,5},{5,4},{6,7},{7,6},{8,9},{9,8},{10,11... | collective-permute-start | bytes 5505032 | tf_op jit(solution)/shard_map/ppermute | solution.py:351
  201.0 11.9 %collective-permute-start.1 = (bf16[8,128,3584]{2,1,0:T(8,128)(2,1)}, bf16[8,128,3584]{2,1,0:T(8,128)(2,1)S(1)}, u32[]{:S(2)}, u32[]{:S(2)}) collective-permute-start(bf16[8,128,3584]{2,1,0:T(8,128)(2,1)} %get-tuple-element.21), channel_id=1, source_target_pairs={{0,1},{1,0},{2,3},{3,2},{4,5},{5,4},{6,7},{7,6},{8,9},{9,8},{10,11... | collective-permute-start | bytes 22020104 | tf_op jit(solution)/shard_map/ppermute | solution.py:364
  212.9 2.9 copy-start.1
  349.3 12.0 %collective-permute-start.2 = (bf16[8,128,3584]{2,1,0:T(8,128)(2,1)}, bf16[8,128,3584]{2,1,0:T(8,128)(2,1)}, u32[]{:S(2)}, u32[]{:S(2)}) collective-permute-start(bf16[8,128,3584]{2,1,0:T(8,128)(2,1)} %get-tuple-element.24), channel_id=1, source_target_pairs={{0,1},{1,0},{2,3},{3,2},{4,5},{5,4},{6,7},{7,6},{8,9},{9,8},{10,11... | collective-permute-start | bytes 22020104 | tf_op jit(solution)/shard_map/ppermute | solution.py:364
  349.4 109.7 %all-to-all-start = ((bf16[8,128,3584]{2,1,0:T(8,128)(2,1)}), bf16[8,128,3584]{2,1,0:T(8,128)(2,1)}, u32[]{:S(2)}, u32[]{:S(2)}) async-start(bf16[8,128,3584]{2,1,0:T(8,128)(2,1)} %add_convert_fusion.1), calls=%async_computation | async-start | bytes 14680064 | tf_op jit(solution)/shard_map/all_to_all | solution.py:370
  459.0 103.4 %all-to-all-start.1 = ((bf16[8,128,3584]{2,1,0:T(8,128)(2,1)}), bf16[8,128,3584]{2,1,0:T(8,128)(2,1)}, u32[]{:S(2)}, u32[]{:S(2)}) async-start(bf16[8,128,3584]{2,1,0:T(8,128)(2,1)} %add_convert_fusion), calls=%async_computation.1 | async-start | bytes 14680064 | tf_op jit(solution)/shard_map/all_to_all | solution.py:370
  558.5 4.0 collective-permute-start.3
  562.5 2.0 copy-start
Sparse Core Ops, SparseCore 0:
  9.6 72.7 all-gather.2
  84.7 69.5 all-gather.4
